TPU v7x, 256 devices: a whole 4x4x8 slice. The times are simulated.
256 devices in a mesh: pop: 16 (over y, z_hi, core), col: 16 (over z_lo, x).
Axes of the slice: x: 4, y: 4, z: 8 (z_hi: 2, z_lo: 4; z = z_hi * 4 + z_lo), core: 2. Of those that a mesh axis runs over, the one named last changes fastest.
Arguments:
- tokens: bfloat16 [14336, 4096], P('pop'), may hold values from -6 to 6
- weight: bfloat16 [4096, 16384], P(None, ('col', 'pop')), may hold values from -0.09375 to 0.09375
- old_left: bfloat16 [1792, 4, 4096], P('pop', None, 'col'), may hold values from -6 to 6
- old_right: bfloat16 [1792, 4, 16384], P('pop', None, 'col'), may hold values from -6 to 6
- selected: int32 [16, 8], P('pop'), may hold values from 0 to 111, as said below
- shaping: float32 [16, 8], P('pop'), may hold values from -3 to 3
- new_left: bfloat16 [1792, 4, 4096], P('pop', None, 'col'), may hold values from -6 to 6
- new_right: bfloat16 [1792, 4, 16384], P('pop', None, 'col'), may hold values from -6 to 6
Outputs:
- updated: bfloat16 [4096, 16384], P(None, ('col', 'pop'))
- activations: bfloat16 [14336, 16384], P('pop', 'col')
Inputs may be any that keep to these rules, and one draw needn't show every extreme that they name: `selected`: each row names 8 different members of its group.
All inputs are finite; a program needn't handle non-finite values.
Results may differ from a plain program's by a relative error of at most 0.0055.
Values may be sent and summed in bfloat16 or wider, within the bound.
A program may use at most 128 MiB of HBM per device.

v0:
```python
import math
import jax
import jax.numpy as jnp
from jax import lax
from jax.sharding import PartitionSpec as P

D = 4096
RANK = 4
noise_scale = 0.5


def laid_out(parts, dim):
    parts = jnp.moveaxis(parts, 0, dim)
    lengths = parts.shape
    return parts.reshape(*lengths[:dim], lengths[dim] * lengths[dim + 1], *lengths[dim + 2 :])


def copy_for_each(x, axis):
    count = lax.axis_size(axis)
    return lax.all_to_all(jnp.broadcast_to(x[None], (count, *x.shape)), axis, 0, 0, tiled=True)


def gather_directly(x, axis, dim):
    return laid_out(copy_for_each(x, axis), dim)


def taken_together(x, axis):
    return copy_for_each(x, axis).sum(axis=0)


def contract_members(left_rows, right_rows):
    return lax.dot_general(
        left_rows, right_rows, (((0,), (0,)), ((), ())), preferred_element_type=jnp.float32
    )


def local(tokens, weight, old_left, old_right, selected, shaping, new_left, new_right):
    groups = lax.axis_size("pop")
    picked = selected[0]
    count = picked.shape[0]
    factor = 1.0 / math.sqrt(D * RANK * count * groups)
    weights_here = shaping[0] * factor
    chosen_left = jnp.take(old_left, picked, axis=0)
    chosen_right = jnp.take(old_right, picked, axis=0)
    scaled_local = (chosen_left.astype(jnp.float32) * weights_here[:, None, None]).astype(
        jnp.bfloat16
    )
    scaled_left = gather_directly(scaled_local, "col", 2)
    every_left = lax.all_gather(scaled_left, "pop", axis=0, tiled=True)
    narrow_right = lax.all_to_all(chosen_right, "pop", split_axis=2, concat_axis=0, tiled=True)
    delta = contract_members(
        every_left.reshape(-1, D), narrow_right.reshape(-1, narrow_right.shape[2])
    )
    updated = (weight.astype(jnp.float32) + delta).astype(jnp.bfloat16)
    base = jnp.dot(
        tokens,
        lax.all_gather(updated, "pop", axis=1, tiled=True),
        preferred_element_type=jnp.float32,
    )
    members_here = new_left.shape[0]
    slab = new_left.shape[2]
    offset = lax.axis_index("col") * slab
    token_slab = lax.dynamic_slice_in_dim(tokens, offset, slab, 1).reshape(members_here, -1, slab)
    partial_proj = jnp.einsum(
        "mtd,mrd->mtr", token_slab, new_left, preferred_element_type=jnp.float32
    )
    proj = taken_together(partial_proj, "col").astype(jnp.bfloat16)
    side = jnp.einsum("mtr,mrh->mth", proj, new_right, preferred_element_type=jnp.float32).reshape(
        base.shape
    )
    pre = base + noise_scale / math.sqrt(D * RANK) * side
    return (updated, (jnp.maximum(pre, 0.0) ** 2).astype(jnp.bfloat16))


def solution(mesh):
    placed = (
        P("pop", None),
        P(None, ("col", "pop")),
        P("pop", None, "col"),
        P("pop", None, "col"),
        P("pop", None),
        P("pop", None),
        P("pop", None, "col"),
        P("pop", None, "col"),
    )
    return jax.shard_map(
        local,
        mesh=mesh,
        in_specs=placed,
        out_specs=(P(None, ("col", "pop")), P("pop", "col")),
        check_vma=False,
    )
```

profile of v0, /device:TPU:1, one launch (start us, length us, event | category | flops | bytes accessed | tf_op | source)
XLA Modules:
  0.0 255.4 jit_solution(2421390312344441921)
XLA Ops:
  7.2 0.0 all-gather.3.cloned.1.call-start
  7.2 0.7 fusion.7
  8.0 0.7 compare_and_fusion
  8.6 0.7 multiply_bitcast_fusion.1
  9.3 1.5 gather_fusion
  10.8 0.1 multiply_convert_fusion
  10.9 18.4 %all_to_all.25 = bf16[16,8,4,256]{3,1,2,0:T(8,128)(2,1)S(1)} all-to-all(bf16[16,8,4,256]{3,1,2,0:T(8,128)(2,1)S(1)} %broadcast_in_dim.35), channel_id=1, replica_groups=mesh['pop'=16,'col'=16] {'col'}, dimensions={0} | all-to-all | bytes 524288 | tf_op jit(solution)/shard_map/all_to_all | solution.py:20
  29.3 0.7 copy.63
  30.0 0.0 all-gather.3.cloned.1.call-update
  30.0 0.0 all-gather.5.cloned.1.call-start
  30.1 1.8 gather_fusion.1
  31.9 0.1 broadcast_select_fusion
  32.0 0.7 copy.57
  32.7 1.1 reshape.88
  33.8 20.4 %all_to_all.26 = bf16[16,2,1024]{2,1,0:T(2,128)(2,1)S(1)} all-to-all(bf16[16,2,1024]{2,1,0:T(2,128)(2,1)S(1)} %reshape.88), channel_id=1, replica_groups=mesh['pop'=16,'col'=16] {'pop'}, dimensions={0} | all-to-all | bytes 131072 | tf_op jit(solution)/shard_map/all_to_all | solution.py:50
  54.2 1.2 reshape.89
  55.4 0.5 copy.58
  56.0 52.5 %all-gather.3.cloned.1.call-done = bf16[128,4,4096]{2,0,1:T(8,128)(2,1)} async-done(((bf16[8,4,4096]{2,0,1:T(8,128)(2,1)}), bf16[128,4,4096]{2,0,1:T(8,128)(2,1)}) %all-gather.3.cloned.1.call-update) | async-done | bytes 4194320 | tf_op jit(solution)/shard_map/all_gather | solution.py:49
  108.5 7.4 %copy.56 = bf16[128,4,4096]{2,1,0:T(4,128)(2,1)} copy(bf16[128,4,4096]{2,0,1:T(8,128)(2,1)} %all-gather.3.cloned.1.call-done) | data formatting | bytes 8388608 | tf_op jit(solution)/shard_map/all_gather | solution.py:49
  115.9 7.0 %reshape.69 = bf16[512,4096]{1,0:T(8,128)(2,1)} reshape(bf16[128,4,4096]{2,1,0:T(4,128)(2,1)} %copy.56) | data formatting | bytes 8388608 | tf_op jit(solution)/shard_map/reshape | solution.py:52
  122.9 3.9 %fusion = bf16[4096,64]{0,1:T(8,128)(2,1)} fusion(bf16[512,4096]{1,0:T(8,128)(2,1)} %reshape.69, bf16[512,64]{1,0:T(8,128)(2,1)S(1)} %bitcast.41, bf16[4096,64]{0,1:T(8,128)(2,1)S(1)} %copy-done.1), kind=kOutput, calls=%fused_computation.3 | convolution fusion | flops 269221888 | bytes 5308416 | tf_op jit(solution)/shard_map/dot_general | solution.py:32
  126.8 0.0 all-gather.5.cloned.1.call-update
  126.8 1.3 fusion.4
  128.1 0.1 copy.59
  128.2 0.1 broadcast_in_dim.38
  128.3 14.1 %all_to_all.27 = f32[16,112,8,4]{1,2,3,0:T(8,128)S(1)} all-to-all(f32[16,112,8,4]{1,2,3,0:T(8,128)S(1)} %broadcast_in_dim.38), channel_id=1, replica_groups=mesh['pop'=16,'col'=16] {'col'}, dimensions={0} | all-to-all | bytes 458752 | tf_op jit(solution)/shard_map/all_to_all | solution.py:20
  142.4 0.2 copy.60
  142.6 2.6 %multiply_bitcast_fusion = f32[896,1024]{1,0:T(8,128)} fusion(bf16[112,8,4]{1,2,0:T(4,128)(2,1)S(1)} %copy.60, bf16[112,4,1024]{2,1,0:T(4,128)(2,1)S(1)} %copy-done), kind=kOutput, calls=%fused_computation.8 | convolution fusion | flops 8257536 | bytes 4594688 | tf_op jit(solution)/shard_map/mtr,mrh->mth/dot_general | solution.py:68
  145.1 5.0 %copy.61 = f32[896,1024]{0,1:T(8,128)} copy(f32[896,1024]{1,0:T(8,128)} %multiply_bitcast_fusion) | data formatting | bytes 7340032 | tf_op jit(solution)/shard_map/mul | solution.py:71
  150.1 81.9 %all-gather.5.cloned.1.call-done = bf16[4096,1024]{0,1:T(8,128)(2,1)} async-done(((bf16[4096,64]{0,1:T(8,128)(2,1)}), bf16[4096,1024]{0,1:T(8,128)(2,1)}) %all-gather.5.cloned.1.call-update) | async-done | bytes 8388624 | tf_op jit(solution)/shard_map/all_gather | solution.py:57
  232.1 14.0 %fusion.3 = bf16[896,1024]{0,1:T(8,128)(2,1)S(1)} fusion(f32[896,1024]{0,1:T(8,128)} %copy.61, bf16[4096,1024]{0,1:T(8,128)(2,1)} %all-gather.5.cloned.1.call-done, bf16[896,4096]{1,0:T(8,128)(2,1)} %param.8), kind=kOutput, calls=%fused_computation.7 | convolution fusion | flops 7519862784 | bytes 21233664 | tf_op jit(solution)/shard_map/dot_general | solution.py:55
  246.1 2.4 copy.62
  (9 shorter events, 0.1 us)
Async XLA Ops:
  7.2 135.4 %copy-start = (bf16[112,4,1024]{2,1,0:T(4,128)(2,1)S(1)}, bf16[112,4,1024]{2,1,0:T(4,128)(2,1)}, u32[]{:S(2)}) copy-start(bf16[112,4,1024]{2,1,0:T(4,128)(2,1)} %param.15) | copy-start | bytes 2752516
  7.2 101.3 %all-gather.3.cloned.1.call-start = ((), (), s32[]{:S(2)}) async-start(), calls=%async_computation.3 | async-start | bytes 4456448 | tf_op jit(solution)/shard_map/all_gather | solution.py:49
  30.0 202.1 %all-gather.5.cloned.1.call-start = ((), (), s32[]{:S(2)}) async-start(), calls=%async_computation.4 | async-start | bytes 8912896 | tf_op jit(solution)/shard_map/all_gather | solution.py:57
  115.9 7.0 %copy-start.1 = (bf16[4096,64]{0,1:T(8,128)(2,1)S(1)}, bf16[4096,64]{0,1:T(8,128)(2,1)}, u32[]{:S(2)}) copy-start(bf16[4096,64]{0,1:T(8,128)(2,1)} %param.9) | copy-start | bytes 1572868
  122.9 3.9 %copy-start.2 = (bf16[112,4,256]{2,1,0:T(4,128)(2,1)S(1)}, bf16[112,4,256]{2,1,0:T(4,128)(2,1)}, u32[]{:S(2)}) copy-start(bf16[112,4,256]{2,1,0:T(4,128)(2,1)} %param.14) | copy-start | bytes 688132
Sparse Core Ops, SparseCore 0:
  30.2 78.3 all-gather.2
  127.0 105.0 all-gather.4
where the time goes:
time: 256 us; the launch traced here: 255 us
  waiting for transfers between devices  135 us (53%)
  blocking collectives  52.9 us (21%)
  local copies, waits for them, and re-layouts  29.7 us (12%)
  matrix products  21.8 us (9%)
  between operations  14.1 us (6%)
    all_gather x1, waiting for transfers between devices, local(): lax.all_gather(updated, 'pop', axis=1, tiled=True)  81.9 us
    all_gather x1, waiting for transfers between devices, local(): every_left = lax.all_gather(scaled_left, 'pop', axis=0, tiled=True)  52.5 us
    all_to_all x2, blocking collectives, copy_for_each(): lax.all_to_all(jnp.broadcast_to(x[None], (count, *x.shape)), axis, 0, 0,...  32.5 us
    all_to_all x1, blocking collectives, local(): lax.all_to_all(chosen_right, 'pop', split_axis=2, concat_axis=0, tiled=True)  20.4 us
    dot_general x1, matrix products, local(): jnp.dot(tokens, lax.all_gather(updated, 'pop', axis=1, tiled=True), prefe...  14 us
    all_gather x1, local copies, waits for them, and re-layouts, local(): every_left = lax.all_gather(scaled_left, 'pop', axis=0, tiled=True)  7.37 us
    reshape x1, local copies, waits for them, and re-layouts, local(): every_left.reshape(-1, D)  7 us
  transfers between devices with their start and end apart: 2, of which 2 were waited for; matrix products, arithmetic and copies ran while one was open for 6% of the time, Pallas kernels for 0%

commit v1 on v0

--- a/solution.py
+++ b/solution.py
@@ -47,7 +47,12 @@
     )
     scaled_left = gather_directly(scaled_local, "col", 2)
     every_left = lax.all_gather(scaled_left, "pop", axis=0, tiled=True)
-    narrow_right = lax.all_to_all(chosen_right, "pop", split_axis=2, concat_axis=0, tiled=True)
+    narrow_right = jnp.concatenate(
+        lax.all_to_all(
+            jnp.stack(jnp.split(chosen_right, lax.axis_size("pop"), axis=2)), "pop", 0, 0
+        ),
+        axis=0,
+    )
     delta = contract_members(
         every_left.reshape(-1, D), narrow_right.reshape(-1, narrow_right.shape[2])
     )

time: 256 us -> 255 us (level)
  transfers between devices with their start and end apart: 2 -> 2, of which waited for: 2 -> 2; matrix products, arithmetic and copies ran while one was open for 6% -> 5% of each run, Pallas kernels for 0% -> 0%
where the time goes in v1:
time: 255 us
  waiting for transfers between devices  137 us (54%)
  blocking collectives  52.8 us (21%)
  local copies, waits for them, and re-layouts  27.2 us (11%)
  matrix products  21.8 us (9%)
  between operations  14.2 us (6%)
    all_gather x1, waiting for transfers between devices, local(): lax.all_gather(updated, 'pop', axis=1, tiled=True)  81.9 us
    all_gather x1, waiting for transfers between devices, local(): every_left = lax.all_gather(scaled_left, 'pop', axis=0, tiled=True)  54.6 us
    all_to_all x2, blocking collectives, copy_for_each(): lax.all_to_all(jnp.broadcast_to(x[None], (count, *x.shape)), axis, 0, 0,...  32.5 us
    all_to_all x1, blocking collectives, local(): lax.all_to_all(jnp.stack(jnp.split(chosen_right, lax.axis_size('pop'), ax...  20.3 us
    dot_general x1, matrix products, local(): jnp.dot(tokens, lax.all_gather(updated, 'pop', axis=1, tiled=True), prefe...  14 us
    all_gather x1, local copies, waits for them, and re-layouts, local(): every_left = lax.all_gather(scaled_left, 'pop', axis=0, tiled=True)  7.37 us
    reshape x1, local copies, waits for them, and re-layouts, local(): every_left.reshape(-1, D)  7 us
  transfers between devices with their start and end apart: 2, of which 2 were waited for; matrix products, arithmetic and copies ran while one was open for 5% of the time, Pallas kernels for 0%

profile of v1, /device:TPU:1, one launch (start us, length us, event | category | flops | bytes accessed | tf_op | source)
XLA Modules:
  0.0 254.8 jit_solution(9738623920727268595)
XLA Ops:
  7.2 0.7 fusion.7
  8.0 0.7 compare_and_fusion
  8.6 0.7 multiply_bitcast_fusion.1
  9.3 1.5 gather_fusion
  10.9 18.4 %all_to_all.15 = bf16[16,8,4,256]{3,1,2,0:T(8,128)(2,1)S(1)} all-to-all(bf16[16,8,4,256]{3,1,2,0:T(8,128)(2,1)S(1)} %broadcast_in_dim.35), channel_id=1, replica_groups=mesh['pop'=16,'col'=16] {'col'}, dimensions={0} | all-to-all | bytes 524288 | tf_op jit(solution)/shard_map/all_to_all | solution.py:20
  29.3 0.7 copy.46
  30.1 1.8 gather_fusion.1
  31.9 0.1 broadcast_select_fusion
  32.0 0.1 constant_dynamic-update-slice_fusion.14
  32.1 0.1 constant_dynamic-update-slice_fusion.12
  32.2 0.1 constant_dynamic-update-slice_fusion.10
  32.3 0.1 constant_dynamic-update-slice_fusion.8
  32.4 0.1 constant_dynamic-update-slice_fusion.6
  32.5 0.1 constant_dynamic-update-slice_fusion.4
  32.6 0.1 constant_dynamic-update-slice_fusion.2
  32.7 0.1 constant_dynamic-update-slice_fusion
  32.8 0.1 reshape.83
  32.9 20.3 %all_to_all.16 = bf16[16,2,1024]{2,1,0:T(2,128)(2,1)S(1)} all-to-all(bf16[16,2,1024]{2,1,0:T(2,128)(2,1)S(1)} %reshape.83), channel_id=1, replica_groups=mesh['pop'=16,'col'=16] {'pop'}, dimensions={0} | all-to-all | bytes 131072 | tf_op jit(solution)/shard_map/all_to_all | solution.py:51
  53.2 0.1 reshape.84
  53.4 54.6 %all-gather.3.cloned.1.call-done = bf16[128,4,4096]{2,0,1:T(8,128)(2,1)} async-done(((bf16[8,4,4096]{2,0,1:T(8,128)(2,1)}), bf16[128,4,4096]{2,0,1:T(8,128)(2,1)}) %all-gather.3.cloned.1.call-update) | async-done | bytes 4194320 | tf_op jit(solution)/shard_map/all_gather | solution.py:49
  108.0 7.4 %copy.41 = bf16[128,4,4096]{2,1,0:T(4,128)(2,1)} copy(bf16[128,4,4096]{2,0,1:T(8,128)(2,1)} %all-gather.3.cloned.1.call-done) | data formatting | bytes 8388608 | tf_op jit(solution)/shard_map/all_gather | solution.py:49
  115.3 7.0 %reshape.65 = bf16[512,4096]{1,0:T(8,128)(2,1)} reshape(bf16[128,4,4096]{2,1,0:T(4,128)(2,1)} %copy.41) | data formatting | bytes 8388608 | tf_op jit(solution)/shard_map/reshape | solution.py:57
  122.3 3.9 %fusion = bf16[4096,64]{0,1:T(8,128)(2,1)} fusion(bf16[512,4096]{1,0:T(8,128)(2,1)} %reshape.65, bf16[512,64]{1,0:T(8,128)(2,1)S(1)} %bitcast.98, bf16[4096,64]{0,1:T(8,128)(2,1)S(1)} %copy-done.1), kind=kOutput, calls=%fused_computation.3 | convolution fusion | flops 269221888 | bytes 5308416 | tf_op jit(solution)/shard_map/dot_general | solution.py:32
  126.3 1.3 fusion.4
  127.6 0.1 copy.42
  127.7 14.1 %all_to_all.17 = f32[16,112,8,4]{1,2,3,0:T(8,128)S(1)} all-to-all(f32[16,112,8,4]{1,2,3,0:T(8,128)S(1)} %broadcast_in_dim.38), channel_id=1, replica_groups=mesh['pop'=16,'col'=16] {'col'}, dimensions={0} | all-to-all | bytes 458752 | tf_op jit(solution)/shard_map/all_to_all | solution.py:20
  141.8 0.2 copy.43
  142.0 2.6 %multiply_bitcast_fusion = f32[896,1024]{1,0:T(8,128)} fusion(bf16[112,8,4]{1,2,0:T(4,128)(2,1)S(1)} %copy.43, bf16[112,4,1024]{2,1,0:T(4,128)(2,1)S(1)} %copy-done), kind=kOutput, calls=%fused_computation.8 | convolution fusion | flops 8257536 | bytes 4594688 | tf_op jit(solution)/shard_map/mtr,mrh->mth/dot_general | solution.py:73
  144.6 5.0 %copy.44 = f32[896,1024]{0,1:T(8,128)} copy(f32[896,1024]{1,0:T(8,128)} %multiply_bitcast_fusion) | data formatting | bytes 7340032 | tf_op jit(solution)/shard_map/mul | solution.py:76
  149.6 81.9 %all-gather.5.cloned.1.call-done = bf16[4096,1024]{0,1:T(8,128)(2,1)} async-done(((bf16[4096,64]{0,1:T(8,128)(2,1)}), bf16[4096,1024]{0,1:T(8,128)(2,1)}) %all-gather.5.cloned.1.call-update) | async-done | bytes 8388624 | tf_op jit(solution)/shard_map/all_gather | solution.py:62
  231.5 14.0 %fusion.3 = bf16[896,1024]{0,1:T(8,128)(2,1)S(1)} fusion(f32[896,1024]{0,1:T(8,128)} %copy.44, bf16[4096,1024]{0,1:T(8,128)(2,1)} %all-gather.5.cloned.1.call-done, bf16[896,4096]{1,0:T(8,128)(2,1)} %param.8), kind=kOutput, calls=%fused_computation.7 | convolution fusion | flops 7519862784 | bytes 21233664 | tf_op jit(solution)/shard_map/dot_general | solution.py:60
  245.6 2.4 copy.45
  (23 shorter events, 0.4 us)
Async XLA Ops:
  7.2 134.8 %copy-start = (bf16[112,4,1024]{2,1,0:T(4,128)(2,1)S(1)}, bf16[112,4,1024]{2,1,0:T(4,128)(2,1)}, u32[]{:S(2)}) copy-start(bf16[112,4,1024]{2,1,0:T(4,128)(2,1)} %param.15) | copy-start | bytes 2752516
  7.2 100.8 %all-gather.3.cloned.1.call-start = ((), (), s32[]{:S(2)}) async-start(), calls=%async_computation.3 | async-start | bytes 4456448 | tf_op jit(solution)/shard_map/all_gather | solution.py:49
  30.0 201.5 %all-gather.5.cloned.1.call-start = ((), (), s32[]{:S(2)}) async-start(), calls=%async_computation.4 | async-start | bytes 8912896 | tf_op jit(solution)/shard_map/all_gather | solution.py:62
  115.3 7.0 %copy-start.1 = (bf16[4096,64]{0,1:T(8,128)(2,1)S(1)}, bf16[4096,64]{0,1:T(8,128)(2,1)}, u32[]{:S(2)}) copy-start(bf16[4096,64]{0,1:T(8,128)(2,1)} %param.9) | copy-start | bytes 1572868
  122.3 3.9 %copy-start.2 = (bf16[112,4,256]{2,1,0:T(4,128)(2,1)S(1)}, bf16[112,4,256]{2,1,0:T(4,128)(2,1)}, u32[]{:S(2)}) copy-start(bf16[112,4,256]{2,1,0:T(4,128)(2,1)} %param.14) | copy-start | bytes 688132
Sparse Core Ops, SparseCore 0:
  30.2 77.7 all-gather.2
  126.4 105.0 all-gather.4
